TPU v7x, 32 devices: a whole 2x2x4 slice. The times are simulated.
32 devices in a mesh: dp: 8 (over z, y), group: 4 (over x, core).
Axes of the slice: x: 2, y: 2, z: 4, core: 2. Of those that a mesh axis runs over, the one named last changes fastest.
Arguments:
- keys: int32 [16384], P(('dp', 'group')), may hold values from 0 to 1073741823
- cut: int32 [1], replicated, may hold values from 256 to 1023
- owner: int32 [16384, 1], P(('dp', 'group')), may hold values from 0 to 7; in each aligned block of 512 rows (0 to 511, 512 to 1023, ...) at most 128 rows name the same one
- tokens: int32 [16384, 2048], P(('dp', 'group')), may hold values from 0 to 128255
Outputs:
- histogram: int32 [4096], replicated
- packed_rows: int32 [32768, 2048], P(('dp', 'group'))
- packed_weights: float32 [32768], P(('dp', 'group'))
Inputs may be any that keep to these rules, and one draw needn't show every extreme that they name: Among the examples of one device, at most 128 have the same owner, and some owner has exactly 128.
All inputs are finite; a program needn't handle non-finite values.
Results may differ from a plain program's by a relative error of at most 0.0003.
Values sent between devices are 32-bit elements; how exact they have to be, the bound alone decides.
A program may use at most 128 MiB of HBM per device.

v0:
```python
import jax
import jax.numpy as jnp
from jax import lax
from jax.sharding import PartitionSpec as P

BINS = 4096
BIN_WIDTH = 262144


def body(keys, cut, owner, tokens):
    examples = keys.shape[0]
    width = tokens.shape[1]
    n_owner = lax.axis_size("dp")
    n_member = lax.axis_size("group")
    slots = 2 * examples // (n_owner * n_member)
    capacity = 2 * examples
    bins_of = keys // BIN_WIDTH
    local_hist = jnp.zeros((BINS,), jnp.float32).at[bins_of].add(1.0)
    kept = bins_of >= cut[0]
    dest = owner[:, 0]
    onehot = (
        (dest[:, None] == jnp.arange(n_owner, dtype=jnp.int32)[None, :]) & kept[:, None]
    ).astype(jnp.int32)
    counts = jnp.sum(onehot, axis=0).astype(jnp.float32)
    table = lax.all_gather(counts[None, :], ("dp", "group"), axis=0, tiled=True)
    position = lax.axis_index(("dp", "group"))
    below = jnp.arange(table.shape[0], dtype=jnp.int32) < position
    before = jnp.sum(jnp.where(below[:, None], table, 0.0), axis=0)
    hist = lax.psum(local_hist, ("dp", "group"))
    running = jnp.cumsum(onehot, axis=0) - onehot
    local_rank = jnp.sum(running * onehot, axis=1)
    offset = jnp.sum(before.astype(jnp.int32)[None, :] * onehot, axis=1)
    rank = offset + local_rank
    member = rank % n_member
    outside = n_owner * n_member * slots
    position_send = jnp.where(
        kept, (dest * n_member + member) * slots + local_rank // n_member, outside
    )
    send_rows = jnp.zeros((outside, width), jnp.int32).at[position_send].set(tokens, mode="drop")
    details = jnp.stack([rank // n_member, keys], axis=1)
    send_meta = jnp.full((outside, 2), -1, jnp.int32).at[position_send].set(details, mode="drop")
    send_rows = send_rows.reshape(n_owner, n_member, slots, width)
    send_meta = send_meta.reshape(n_owner, n_member, slots, 2)
    got_rows, got_meta = (
        lax.all_to_all(
            lax.all_to_all(send_rows, "dp", split_axis=0, concat_axis=0, tiled=True),
            "group",
            split_axis=1,
            concat_axis=1,
            tiled=True,
        ),
        lax.all_to_all(
            lax.all_to_all(send_meta, "dp", split_axis=0, concat_axis=0, tiled=True),
            "group",
            split_axis=1,
            concat_axis=1,
            tiled=True,
        ),
    )
    got_rows = got_rows.reshape(-1, width)
    got_meta = got_meta.reshape(-1, 2)
    slot = got_meta[:, 0]
    valid = slot >= 0
    target = jnp.where(valid, slot, capacity)
    suffix = jnp.cumsum(hist[::-1])[::-1]
    total = jnp.maximum(suffix[cut[0]], 1.0)
    got_bins = jnp.clip(got_meta[:, 1] // BIN_WIDTH, 0, BINS - 1)
    weight = jnp.where(valid, suffix[got_bins] / total, 0.0)
    packed_rows = jnp.zeros((capacity, width), jnp.int32).at[target].set(got_rows, mode="drop")
    packed_weights = jnp.zeros((capacity,), jnp.float32).at[target].set(weight, mode="drop")
    return (hist.astype(jnp.int32), packed_rows, packed_weights)


def solution(mesh):
    placed = (P(("dp", "group")), P(), P(("dp", "group"), None), P(("dp", "group"), None))
    return jax.shard_map(
        body,
        mesh=mesh,
        in_specs=placed,
        out_specs=(P(), P(("dp", "group"), None), P(("dp", "group"))),
        check_vma=False,
    )
```

profile of v0, /device:TPU:0, one launch (start us, length us, event | category | flops | bytes accessed | tf_op | source)
XLA Modules:
  0.0 387.2 jit_solution(11714940786831163853)
XLA Ops:
  1.3 0.7 broadcast_compare_fusion
  2.0 0.8 convert_reduce_fusion
  2.8 3.3 scatter_custom_fusion
  6.2 42.1 %all-reduce.1 = (f32[4096]{0:T(1024)S(1)}, f32[256]{0:T(256)S(1)}) all-reduce(f32[4096]{0:T(1024)S(1)} %scatter_custom_fusion, f32[256]{0:T(256)S(1)} %convert_dynamic-update-slice_fusion), channel_id=1, replica_groups=mesh['dp'=8,'group'=4] {'dp','group'}, use_global_device_ids=true, to_apply=%region_1.2 | all-reduce | flops 4352 | bytes 34816 | tf_op jit(solution)/shard_map/psum | solution.py:29
  48.5 0.7 fusion.10
  49.2 1.1 reduce-window.15
  50.6 0.8 select_reduce_fusion
  51.4 0.7 compare_select_fusion.6
  52.1 0.7 pad_add_fusion
  52.9 1.8 scatter_custom_fusion.1
  55.0 0.7 reshape.203
  55.7 5.3 %all-to-all-start = ((s32[8,1,256]{2,1,0:T(1,128)}), s32[8,1,256]{2,1,0:T(1,128)S(1)}, u32[]{:S(2)}, u32[]{:S(2)}) async-start(s32[8,1,256]{2,1,0:T(1,128)} %reshape.203), calls=%async_computation | async-start | bytes 16384 | tf_op jit(solution)/shard_map/all_to_all | solution.py:53
  61.1 8.6 %scatter_custom_fusion.2 = s32[1024,2048]{1,0:T(8,128)} fusion(s32[512]{0:T(512)S(1)} %get-tuple-element.7, s32[512,2048]{1,0:T(8,128)} %param.7, s32[]{:T(128)} %constant.83.clone.1), kind=kCustom, calls=%fused_computation.8 | custom fusion | bytes 8389120 | tf_op jit(solution)/shard_map/scatter | solution.py:39
  69.7 6.0 %all-to-all-start.2 = ((s32[8,4,32,2048]{3,2,1,0:T(8,128)}), s32[8,4,32,2048]{3,2,1,0:T(8,128)}, u32[]{:S(2)}, u32[]{:S(2)}) async-start(s32[8,4,32,2048]{3,2,1,0:T(8,128)} %bitcast.35), calls=%async_computation.2 | async-start | bytes 16777216 | tf_op jit(solution)/shard_map/all_to_all | solution.py:46
  76.9 0.7 reshape.205
  77.5 179.0 %all-to-all-done.2 = s32[8,4,32,2048]{3,2,1,0:T(8,128)} async-done(((s32[8,4,32,2048]{3,2,1,0:T(8,128)}), s32[8,4,32,2048]{3,2,1,0:T(8,128)}, u32[]{:S(2)}, u32[]{:S(2)}) %all-to-all-start.2) | async-done | bytes 8388640 | tf_op jit(solution)/shard_map/all_to_all | solution.py:46
  256.5 3.2 all-to-all-start.1
  259.8 7.9 %copy.23 = s32[8,4,32,2048]{3,2,0,1:T(8,128)} copy(s32[8,4,32,2048]{3,2,1,0:T(8,128)} %all-to-all-done.2) | data formatting | bytes 16777216 | tf_op jit(solution)/shard_map/all_to_all | solution.py:46
  267.7 5.7 %all-to-all-start.3 = ((s32[8,4,32,2048]{3,2,0,1:T(8,128)}), s32[8,4,32,2048]{3,2,0,1:T(8,128)}, u32[]{:S(2)}, u32[]{:S(2)}) async-start(s32[8,4,32,2048]{3,2,0,1:T(8,128)} %copy.23), calls=%async_computation.3 | async-start | bytes 16777216 | tf_op jit(solution)/shard_map/all_to_all | solution.py:45
  276.8 6.2 %gather_fusion = f32[1024]{0:T(1024)S(1)} fusion(f32[4096]{0:T(1024)S(1)} %rev.7, s32[1024]{0:T(1024)S(1)} %broadcast_clamp_fusion), kind=kCustom, calls=%fused_computation | custom fusion | bytes 12288 | tf_op jit(solution)/shard_map/gather | solution.py:68
  283.0 4.9 %scatter_custom_fusion.4 = f32[1024]{0:T(1024)} fusion(s32[1024]{0:T(1024)S(1)} %bitcast.51, f32[1024]{0:T(1024)S(1)} %divide_select_fusion, f32[]{:T(128)} %constant.81.clone.1), kind=kCustom, calls=%fused_computation.63 | custom fusion | bytes 4100 | tf_op jit(solution)/shard_map/scatter | solution.py:70
  287.9 78.6 %all-to-all-done.3 = s32[8,4,32,2048]{3,2,0,1:T(8,128)} async-done(((s32[8,4,32,2048]{3,2,0,1:T(8,128)}), s32[8,4,32,2048]{3,2,0,1:T(8,128)}, u32[]{:S(2)}, u32[]{:S(2)}) %all-to-all-start.3) | async-done | bytes 8388640 | tf_op jit(solution)/shard_map/all_to_all | solution.py:45
  366.5 7.7 %copy.24 = s32[8,4,32,2048]{3,2,1,0:T(8,128)} copy(s32[8,4,32,2048]{3,2,0,1:T(8,128)} %all-to-all-done.3) | data formatting | bytes 16777216 | tf_op jit(solution)/shard_map/all_to_all | solution.py:45
  374.2 13.0 %scatter_custom_fusion.3 = s32[1024,2048]{1,0:T(8,128)} fusion(s32[1024]{0:T(1024)S(1)} %bitcast.52, s32[1024,2048]{1,0:T(8,128)} %bitcast.36, s32[]{:T(128)} %constant.83.clone.1), kind=kCustom, calls=%fused_computation.6 | custom fusion | bytes 8389120 | tf_op jit(solution)/shard_map/scatter | solution.py:69
  (37 shorter events, 5.0 us)
Async XLA Ops:
  55.7 13.9 %all-to-all-start = ((s32[8,1,256]{2,1,0:T(1,128)}), s32[8,1,256]{2,1,0:T(1,128)S(1)}, u32[]{:S(2)}, u32[]{:S(2)}) async-start(s32[8,1,256]{2,1,0:T(1,128)} %reshape.203), calls=%async_computation | async-start | bytes 16384 | tf_op jit(solution)/shard_map/all_to_all | solution.py:53
  69.7 186.9 %all-to-all-start.2 = ((s32[8,4,32,2048]{3,2,1,0:T(8,128)}), s32[8,4,32,2048]{3,2,1,0:T(8,128)}, u32[]{:S(2)}, u32[]{:S(2)}) async-start(s32[8,4,32,2048]{3,2,1,0:T(8,128)} %bitcast.35), calls=%async_computation.2 | async-start | bytes 16777216 | tf_op jit(solution)/shard_map/all_to_all | solution.py:46
  256.5 11.1 %all-to-all-start.1 = ((s32[4,1,512]{2,1,0:T(1,128)}), s32[4,1,512]{2,1,0:T(1,128)S(1)}, u32[]{:S(2)}, u32[]{:S(2)}) async-start(s32[4,1,512]{2,1,0:T(1,128)} %reshape.205), calls=%async_computation.1 | async-start | bytes 16384 | tf_op jit(solution)/shard_map/all_to_all | solution.py:52
  267.7 98.8 %all-to-all-start.3 = ((s32[8,4,32,2048]{3,2,0,1:T(8,128)}), s32[8,4,32,2048]{3,2,0,1:T(8,128)}, u32[]{:S(2)}, u32[]{:S(2)}) async-start(s32[8,4,32,2048]{3,2,0,1:T(8,128)} %copy.23), calls=%async_computation.3 | async-start | bytes 16777216 | tf_op jit(solution)/shard_map/all_to_all | solution.py:45
where the time goes:
time: 388 us; the launch traced here: 387 us
  waiting for transfers between devices  258 us (66%)
  local copies, waits for them, and re-layouts  53.9 us (14%)
  blocking collectives  42.1 us (11%)
  starting transfers between devices  20.2 us (5%)
  other arithmetic  11.3 us (3%)
    all_to_all x1, waiting for transfers between devices, body(): lax.all_to_all(send_rows, 'dp', split_axis=0, concat_axis=0, tiled=True)  179 us
    all_to_all x1, waiting for transfers between devices, body(): lax.all_to_all(lax.all_to_all(send_rows, 'dp', split_axis=0, concat_axis=...  78.6 us
    psum x1, blocking collectives, body(): hist = lax.psum(local_hist, ('dp', 'group'))  42.1 us
    scatter x1, local copies, waits for them, and re-layouts, body(): jnp.zeros((capacity, width), jnp.int32).at[target]  13 us
    scatter x1, local copies, waits for them, and re-layouts, body(): jnp.zeros((outside, width), jnp.int32).at[position_send]  8.6 us
    all_to_all x1, local copies, waits for them, and re-layouts, body(): lax.all_to_all(send_rows, 'dp', split_axis=0, concat_axis=0, tiled=True)  7.89 us
  transfers between devices with their start and end apart: 4, of which 2 were waited for; matrix products, arithmetic and copies ran while one was open for 8% of the time, Pallas kernels for 0%

commit v1 on v0

--- a/solution.py
+++ b/solution.py
@@ -26,7 +26,7 @@
     position = lax.axis_index(("dp", "group"))
     below = jnp.arange(table.shape[0], dtype=jnp.int32) < position
     before = jnp.sum(jnp.where(below[:, None], table, 0.0), axis=0)
-    hist = lax.psum(local_hist, ("dp", "group"))
+    hist = lax.psum(lax.psum(local_hist, "group"), "dp")
     running = jnp.cumsum(onehot, axis=0) - onehot
     local_rank = jnp.sum(running * onehot, axis=1)
     offset = jnp.sum(before.astype(jnp.int32)[None, :] * onehot, axis=1)

time: 388 us -> 440 us (1.13)
  blocking collectives: 42.1 us -> 173 us
  waiting for transfers between devices: 258 us -> 179 us
    psum x1 -> x2, blocking collectives: 42.1 us -> 131 us  [body(): hist = lax.psum(lax.psum(local_hist, 'group'), 'dp')]
    all_to_all x1, waiting for transfers between devices: 78.6 us -> 0.01 us  [body(): lax.all_to_all(lax.all_to_all(send_rows, 'dp', split_axis=0, concat_axis=...]
    unnamed x0 -> x1, blocking collectives: none -> 41.9 us
  transfers between devices with their start and end apart: 4 -> 4, of which waited for: 2 -> 1; matrix products, arithmetic and copies ran while one was open for 8% -> 8% of each run, Pallas kernels for 0% -> 0%
where the time goes in v1:
time: 440 us; the launch traced here: 439 us
  waiting for transfers between devices  179 us (41%)
  blocking collectives  173 us (39%)
  local copies, waits for them, and re-layouts  53.9 us (12%)
  starting transfers between devices  20.2 us (5%)
  other arithmetic  11.3 us (3%)
    all_to_all x1, waiting for transfers between devices, body(): lax.all_to_all(send_rows, 'dp', split_axis=0, concat_axis=0, tiled=True)  179 us
    psum x2, blocking collectives, body(): hist = lax.psum(lax.psum(local_hist, 'group'), 'dp')  131 us
    unnamed x1, blocking collectives  41.9 us
    scatter x1, local copies, waits for them, and re-layouts, body(): jnp.zeros((capacity, width), jnp.int32).at[target]  13 us
  transfers between devices with their start and end apart: 4, of which 1 were waited for; matrix products, arithmetic and copies ran while one was open for 8% of the time, Pallas kernels for 0%

profile of v1, /device:TPU:0, one launch (start us, length us, event | category | flops | bytes accessed | tf_op | source)
XLA Modules:
  0.0 439.3 jit_solution(8992049857521741574)
XLA Ops:
  1.3 0.7 broadcast_compare_fusion
  2.0 0.8 convert_reduce_fusion
  2.9 41.9 %all-reduce = f32[256]{0:T(256)S(1)} all-reduce(f32[256]{0:T(256)S(1)} %convert_dynamic-update-slice_fusion), channel_id=2, replica_groups=mesh['dp'=8,'group'=4] {'dp','group'}, use_global_device_ids=true, to_apply=%add | all-reduce | flops 256 | bytes 2048
  45.0 0.7 fusion.10
  45.7 1.1 reduce-window.15
  47.1 0.8 select_reduce_fusion
  47.9 0.7 compare_select_fusion.6
  48.6 0.7 pad_add_fusion
  49.4 1.8 scatter_custom_fusion.1
  51.5 0.7 reshape.203
  52.3 5.3 %all-to-all-start = ((s32[8,1,256]{2,1,0:T(1,128)}), s32[8,1,256]{2,1,0:T(1,128)S(1)}, u32[]{:S(2)}, u32[]{:S(2)}) async-start(s32[8,1,256]{2,1,0:T(1,128)} %reshape.203), calls=%async_computation | async-start | bytes 16384 | tf_op jit(solution)/shard_map/all_to_all | solution.py:53
  57.6 8.6 %scatter_custom_fusion.2 = s32[1024,2048]{1,0:T(8,128)} fusion(s32[512]{0:T(512)S(1)} %get-tuple-element.5, s32[512,2048]{1,0:T(8,128)} %param.7, s32[]{:T(128)} %constant.83.clone.1), kind=kCustom, calls=%fused_computation.8 | custom fusion | bytes 8389120 | tf_op jit(solution)/shard_map/scatter | solution.py:39
  66.2 6.0 %all-to-all-start.2 = ((s32[8,4,32,2048]{3,2,1,0:T(8,128)}), s32[8,4,32,2048]{3,2,1,0:T(8,128)}, u32[]{:S(2)}, u32[]{:S(2)}) async-start(s32[8,4,32,2048]{3,2,1,0:T(8,128)} %bitcast.31), calls=%async_computation.2 | async-start | bytes 16777216 | tf_op jit(solution)/shard_map/all_to_all | solution.py:46
  74.0 179.0 %all-to-all-done.2 = s32[8,4,32,2048]{3,2,1,0:T(8,128)} async-done(((s32[8,4,32,2048]{3,2,1,0:T(8,128)}), s32[8,4,32,2048]{3,2,1,0:T(8,128)}, u32[]{:S(2)}, u32[]{:S(2)}) %all-to-all-start.2) | async-done | bytes 8388640 | tf_op jit(solution)/shard_map/all_to_all | solution.py:46
  253.0 3.2 all-to-all-start.1
  256.3 7.9 %copy.23 = s32[8,4,32,2048]{3,2,0,1:T(8,128)} copy(s32[8,4,32,2048]{3,2,1,0:T(8,128)} %all-to-all-done.2) | data formatting | bytes 16777216 | tf_op jit(solution)/shard_map/all_to_all | solution.py:46
  264.2 5.7 %all-to-all-start.3 = ((s32[8,4,32,2048]{3,2,0,1:T(8,128)}), s32[8,4,32,2048]{3,2,0,1:T(8,128)}, u32[]{:S(2)}, u32[]{:S(2)}) async-start(s32[8,4,32,2048]{3,2,0,1:T(8,128)} %copy.23), calls=%async_computation.3 | async-start | bytes 16777216 | tf_op jit(solution)/shard_map/all_to_all | solution.py:45
  269.9 3.3 scatter_custom_fusion
  273.1 95.6 %psum.14 = f32[4096]{0:T(1024)S(1)} all-reduce(f32[4096]{0:T(1024)S(1)} %scatter_custom_fusion), channel_id=1, replica_groups=mesh['dp'=8,'group'=4] {'group'}, use_global_device_ids=true, to_apply=%region_1.2 | all-reduce | flops 4096 | bytes 32768 | tf_op jit(solution)/shard_map/psum | solution.py:29
  368.8 35.2 %psum.15 = f32[4096]{0:T(1024)S(1)} all-reduce(f32[4096]{0:T(1024)S(1)} %psum.14), channel_id=1, replica_groups=mesh['dp'=8,'group'=4] {'dp'}, use_global_device_ids=true, to_apply=%region_2.3 | all-reduce | flops 4096 | bytes 32768 | tf_op jit(solution)/shard_map/psum | solution.py:29
  407.4 6.2 %gather_fusion = f32[1024]{0:T(1024)S(1)} fusion(f32[4096]{0:T(1024)S(1)} %rev.7, s32[1024]{0:T(1024)S(1)} %broadcast_clamp_fusion), kind=kCustom, calls=%fused_computation | custom fusion | bytes 12288 | tf_op jit(solution)/shard_map/gather | solution.py:68
  413.6 4.9 %scatter_custom_fusion.4 = f32[1024]{0:T(1024)} fusion(s32[1024]{0:T(1024)S(1)} %bitcast.47, f32[1024]{0:T(1024)S(1)} %divide_select_fusion, f32[]{:T(128)} %constant.81.clone.1), kind=kCustom, calls=%fused_computation.63 | custom fusion | bytes 4100 | tf_op jit(solution)/shard_map/scatter | solution.py:70
  418.5 7.7 %copy.24 = s32[8,4,32,2048]{3,2,1,0:T(8,128)} copy(s32[8,4,32,2048]{3,2,0,1:T(8,128)} %all-to-all-done.3) | data formatting | bytes 16777216 | tf_op jit(solution)/shard_map/all_to_all | solution.py:45
  426.2 13.0 %scatter_custom_fusion.3 = s32[1024,2048]{1,0:T(8,128)} fusion(s32[1024]{0:T(1024)S(1)} %bitcast.48, s32[1024,2048]{1,0:T(8,128)} %bitcast.32, s32[]{:T(128)} %constant.83.clone.1), kind=kCustom, calls=%fused_computation.6 | custom fusion | bytes 8389120 | tf_op jit(solution)/shard_map/scatter | solution.py:69
  (39 shorter events, 5.7 us)
Async XLA Ops:
  52.3 13.9 %all-to-all-start = ((s32[8,1,256]{2,1,0:T(1,128)}), s32[8,1,256]{2,1,0:T(1,128)S(1)}, u32[]{:S(2)}, u32[]{:S(2)}) async-start(s32[8,1,256]{2,1,0:T(1,128)} %reshape.203), calls=%async_computation | async-start | bytes 16384 | tf_op jit(solution)/shard_map/all_to_all | solution.py:53
  66.2 186.9 %all-to-all-start.2 = ((s32[8,4,32,2048]{3,2,1,0:T(8,128)}), s32[8,4,32,2048]{3,2,1,0:T(8,128)}, u32[]{:S(2)}, u32[]{:S(2)}) async-start(s32[8,4,32,2048]{3,2,1,0:T(8,128)} %bitcast.31), calls=%async_computation.2 | async-start | bytes 16777216 | tf_op jit(solution)/shard_map/all_to_all | solution.py:46
  253.0 11.1 %all-to-all-start.1 = ((s32[4,1,512]{2,1,0:T(1,128)}), s32[4,1,512]{2,1,0:T(1,128)S(1)}, u32[]{:S(2)}, u32[]{:S(2)}) async-start(s32[4,1,512]{2,1,0:T(1,128)} %reshape.205), calls=%async_computation.1 | async-start | bytes 16384 | tf_op jit(solution)/shard_map/all_to_all | solution.py:52
  264.2 154.3 %all-to-all-start.3 = ((s32[8,4,32,2048]{3,2,0,1:T(8,128)}), s32[8,4,32,2048]{3,2,0,1:T(8,128)}, u32[]{:S(2)}, u32[]{:S(2)}) async-start(s32[8,4,32,2048]{3,2,0,1:T(8,128)} %copy.23), calls=%async_computation.3 | async-start | bytes 16777216 | tf_op jit(solution)/shard_map/all_to_all | solution.py:45

commit v2 on v0

--- a/solution.py
+++ b/solution.py
@@ -26,7 +26,7 @@
     position = lax.axis_index(("dp", "group"))
     below = jnp.arange(table.shape[0], dtype=jnp.int32) < position
     before = jnp.sum(jnp.where(below[:, None], table, 0.0), axis=0)
-    hist = lax.psum(local_hist, ("dp", "group"))
+    hist = jnp.sum(lax.all_gather(local_hist, ("dp", "group")), axis=0)
     running = jnp.cumsum(onehot, axis=0) - onehot
     local_rank = jnp.sum(running * onehot, axis=1)
     offset = jnp.sum(before.astype(jnp.int32)[None, :] * onehot, axis=1)

time: 388 us -> 432 us (1.11)
  blocking collectives: 42.1 us -> 164 us
  waiting for transfers between devices: 258 us -> 179 us
    all_gather x0 -> x1, blocking collectives: none -> 122 us  [body(): hist = jnp.sum(lax.all_gather(local_hist, ('dp', 'group')), axis=0)]
    all_to_all x1, waiting for transfers between devices: 78.6 us -> 0.01 us  [body(): lax.all_to_all(lax.all_to_all(send_rows, 'dp', split_axis=0, concat_axis=...]
    psum x1 -> x0, blocking collectives: 42.1 us -> none  [body(): hist = lax.psum(local_hist, ('dp', 'group'))]
    unnamed x0 -> x1, blocking collectives: none -> 41.9 us
  transfers between devices with their start and end apart: 4 -> 4, of which waited for: 2 -> 1; matrix products, arithmetic and copies ran while one was open for 8% -> 8% of each run, Pallas kernels for 0% -> 0%
where the time goes in v2:
time: 432 us; the launch traced here: 431 us
  waiting for transfers between devices  179 us (41%)
  blocking collectives  164 us (38%)
  local copies, waits for them, and re-layouts  54 us (12%)
  starting transfers between devices  20.2 us (5%)
  other arithmetic  11.3 us (3%)
    all_to_all x1, waiting for transfers between devices, body(): lax.all_to_all(send_rows, 'dp', split_axis=0, concat_axis=0, tiled=True)  179 us
    all_gather x1, blocking collectives, body(): hist = jnp.sum(lax.all_gather(local_hist, ('dp', 'group')), axis=0)  122 us
    unnamed x1, blocking collectives  41.9 us
    scatter x1, local copies, waits for them, and re-layouts, body(): jnp.zeros((capacity, width), jnp.int32).at[target]  13 us
  transfers between devices with their start and end apart: 4, of which 1 were waited for; matrix products, arithmetic and copies ran while one was open for 8% of the time, Pallas kernels for 0%

profile of v2, /device:TPU:0, one launch (start us, length us, event | category | flops | bytes accessed | tf_op | source)
XLA Modules:
  0.0 430.8 jit_solution(2945740407947892639)
XLA Ops:
  1.3 0.7 broadcast_compare_fusion
  2.0 0.8 convert_reduce_fusion
  2.9 41.9 %all-reduce = f32[256]{0:T(256)S(1)} all-reduce(f32[256]{0:T(256)S(1)} %convert_dynamic-update-slice_fusion), channel_id=3, replica_groups=mesh['dp'=8,'group'=4] {'dp','group'}, use_global_device_ids=true, to_apply=%add | all-reduce | flops 256 | bytes 2048
  45.0 0.7 fusion.10
  45.7 1.1 reduce-window.15
  47.1 0.8 select_reduce_fusion
  47.9 0.7 compare_select_fusion.6
  48.6 0.7 pad_add_fusion
  49.4 1.8 scatter_custom_fusion.1
  51.5 0.7 reshape.204
  52.3 5.3 %all-to-all-start = ((s32[8,1,256]{2,1,0:T(1,128)}), s32[8,1,256]{2,1,0:T(1,128)S(1)}, u32[]{:S(2)}, u32[]{:S(2)}) async-start(s32[8,1,256]{2,1,0:T(1,128)} %reshape.204), calls=%async_computation | async-start | bytes 16384 | tf_op jit(solution)/shard_map/all_to_all | solution.py:53
  57.6 8.6 %scatter_custom_fusion.2 = s32[1024,2048]{1,0:T(8,128)} fusion(s32[512]{0:T(512)S(1)} %get-tuple-element.5, s32[512,2048]{1,0:T(8,128)} %param.7, s32[]{:T(128)} %constant.83.clone.1), kind=kCustom, calls=%fused_computation.8 | custom fusion | bytes 8389120 | tf_op jit(solution)/shard_map/scatter | solution.py:39
  66.2 6.0 %all-to-all-start.2 = ((s32[8,4,32,2048]{3,2,1,0:T(8,128)}), s32[8,4,32,2048]{3,2,1,0:T(8,128)}, u32[]{:S(2)}, u32[]{:S(2)}) async-start(s32[8,4,32,2048]{3,2,1,0:T(8,128)} %bitcast.31), calls=%async_computation.2 | async-start | bytes 16777216 | tf_op jit(solution)/shard_map/all_to_all | solution.py:46
  73.3 0.7 reshape.206
  74.0 179.0 %all-to-all-done.2 = s32[8,4,32,2048]{3,2,1,0:T(8,128)} async-done(((s32[8,4,32,2048]{3,2,1,0:T(8,128)}), s32[8,4,32,2048]{3,2,1,0:T(8,128)}, u32[]{:S(2)}, u32[]{:S(2)}) %all-to-all-start.2) | async-done | bytes 8388640 | tf_op jit(solution)/shard_map/all_to_all | solution.py:46
  253.0 3.2 all-to-all-start.1
  256.3 7.9 %copy.29 = s32[8,4,32,2048]{3,2,0,1:T(8,128)} copy(s32[8,4,32,2048]{3,2,1,0:T(8,128)} %all-to-all-done.2) | data formatting | bytes 16777216 | tf_op jit(solution)/shard_map/all_to_all | solution.py:46
  264.2 5.7 %all-to-all-start.3 = ((s32[8,4,32,2048]{3,2,0,1:T(8,128)}), s32[8,4,32,2048]{3,2,0,1:T(8,128)}, u32[]{:S(2)}, u32[]{:S(2)}) async-start(s32[8,4,32,2048]{3,2,0,1:T(8,128)} %copy.29), calls=%async_computation.3 | async-start | bytes 16777216 | tf_op jit(solution)/shard_map/all_to_all | solution.py:45
  269.9 3.3 scatter_custom_fusion
  273.1 122.2 %all-gather = f32[131072]{0:T(1024)S(1)} all-gather(f32[4096]{0:T(1024)S(1)} %scatter_custom_fusion), channel_id=2, replica_groups=mesh['dp'=8,'group'=4] {'dp','group'}, dimensions={0}, use_global_device_ids=true | all-gather | bytes 540672 | tf_op jit(solution)/shard_map/all_gather | solution.py:29
  399.0 6.2 %gather_fusion = f32[1024]{0:T(1024)S(1)} fusion(f32[4096]{0:T(1024)S(1)} %rev.7, s32[1024]{0:T(1024)S(1)} %broadcast_clamp_fusion), kind=kCustom, calls=%fused_computation | custom fusion | bytes 12288 | tf_op jit(solution)/shard_map/gather | solution.py:68
  405.2 4.9 %scatter_custom_fusion.4 = f32[1024]{0:T(1024)} fusion(s32[1024]{0:T(1024)S(1)} %bitcast.47, f32[1024]{0:T(1024)S(1)} %divide_select_fusion, f32[]{:T(128)} %constant.81.clone.1), kind=kCustom, calls=%fused_computation.63 | custom fusion | bytes 4100 | tf_op jit(solution)/shard_map/scatter | solution.py:70
  410.0 7.7 %copy.30 = s32[8,4,32,2048]{3,2,1,0:T(8,128)} copy(s32[8,4,32,2048]{3,2,0,1:T(8,128)} %all-to-all-done.3) | data formatting | bytes 16777216 | tf_op jit(solution)/shard_map/all_to_all | solution.py:45
  417.7 13.0 %scatter_custom_fusion.3 = s32[1024,2048]{1,0:T(8,128)} fusion(s32[1024]{0:T(1024)S(1)} %bitcast.48, s32[1024,2048]{1,0:T(8,128)} %bitcast.32, s32[]{:T(128)} %constant.83.clone.1), kind=kCustom, calls=%fused_computation.6 | custom fusion | bytes 8389120 | tf_op jit(solution)/shard_map/scatter | solution.py:69
  (40 shorter events, 5.1 us)
Async XLA Ops:
  52.3 13.9 %all-to-all-start = ((s32[8,1,256]{2,1,0:T(1,128)}), s32[8,1,256]{2,1,0:T(1,128)S(1)}, u32[]{:S(2)}, u32[]{:S(2)}) async-start(s32[8,1,256]{2,1,0:T(1,128)} %reshape.204), calls=%async_computation | async-start | bytes 16384 | tf_op jit(solution)/shard_map/all_to_all | solution.py:53
  66.2 186.9 %all-to-all-start.2 = ((s32[8,4,32,2048]{3,2,1,0:T(8,128)}), s32[8,4,32,2048]{3,2,1,0:T(8,128)}, u32[]{:S(2)}, u32[]{:S(2)}) async-start(s32[8,4,32,2048]{3,2,1,0:T(8,128)} %bitcast.31), calls=%async_computation.2 | async-start | bytes 16777216 | tf_op jit(solution)/shard_map/all_to_all | solution.py:46
  253.0 11.1 %all-to-all-start.1 = ((s32[4,1,512]{2,1,0:T(1,128)}), s32[4,1,512]{2,1,0:T(1,128)S(1)}, u32[]{:S(2)}, u32[]{:S(2)}) async-start(s32[4,1,512]{2,1,0:T(1,128)} %reshape.206), calls=%async_computation.1 | async-start | bytes 16384 | tf_op jit(solution)/shard_map/all_to_all | solution.py:52
  264.2 145.9 %all-to-all-start.3 = ((s32[8,4,32,2048]{3,2,0,1:T(8,128)}), s32[8,4,32,2048]{3,2,0,1:T(8,128)}, u32[]{:S(2)}, u32[]{:S(2)}) async-start(s32[8,4,32,2048]{3,2,0,1:T(8,128)} %copy.29), calls=%async_computation.3 | async-start | bytes 16777216 | tf_op jit(solution)/shard_map/all_to_all | solution.py:45
